TPU v7x, 512 devices: a whole 4x4x16 slice. The times are simulated.
512 devices in a mesh: rep: 4 (over y_hi, core), shard: 128 (over y_lo, z, x).
Axes of the slice: x: 4, y: 4 (y_hi: 2, y_lo: 2; y = y_hi * 2 + y_lo), z: 16, core: 2. Of those that a mesh axis runs over, the one named last changes fastest.
Arguments:
- gradients: float32 [4, 128, 8, 5120], P('rep', 'shard'), may hold values from -6 to 6
- master: float32 [128, 8, 5120], P('shard', 'rep'), may hold values from -6 to 6
- first_moment: float32 [128, 8, 5120], P('shard', 'rep'), may hold values from -4 to 4
- second_moment: float32 [128, 8, 5120], P('shard', 'rep'), may hold values from 0.001 to 0.01
- old_ratio: float32 [128], replicated, may hold values from 0.5 to 2
- group_owner: int32 [128], replicated, may hold values from 0 to 127, each once
- layer_group: int32 [128], replicated, may hold values from 0 to 127, each once
Outputs:
- new_master: float32 [128, 8, 5120], P('shard', 'rep')
- new_first: float32 [128, 8, 5120], P('shard', 'rep')
- new_second: float32 [128, 8, 5120], P('shard', 'rep')
- replica: bfloat16 [128, 8, 5120], P(None, 'rep')
- new_ratio: float32 [128], replicated
Inputs may be any that keep to these rules, and one draw needn't show every extreme that they name: `group_owner`: every device owns exactly one group. `layer_group`: every group holds exactly one layer.
All inputs are finite; a program needn't handle non-finite values.
Results may differ from a plain program's by a relative error of at most 0.0004.
Values may be sent and summed in bfloat16 or wider, within the bound.
A program may use at most 64 MiB of HBM per device.

v0:
```python
import jax
import jax.numpy as jnp
from jax import lax
from jax.sharding import Mesh
from jax.sharding import PartitionSpec as P

REP = ("rep_0", "rep_1")
SHARD = ("shard_0", "shard_1", "shard_2")
REP_SHARD = ("rep_0", "rep_1", "shard_0", "shard_1", "shard_2")


def in_blocks(x, dim, count):
    before, after = (x.shape[:dim], x.shape[dim + 1 :])
    return jnp.moveaxis(x.reshape(*before, count, -1, *after), dim, 0)


def sum_at_owner(x, axis, dim):
    tiles = in_blocks(x, dim, lax.axis_size(axis))
    arrived = lax.all_to_all(tiles, axis, split_axis=0, concat_axis=0, tiled=True)
    return arrived.sum(axis=0)


def over_axes(x, axes):
    for axis in axes:
        x = lax.psum(x, axis)
    return x


def joined_along(tiles, dim):
    shape = list(tiles.shape[1:])
    shape[dim] *= tiles.shape[0]
    return jnp.moveaxis(tiles, 0, dim).reshape(shape)


def gather_in_order(x, axes, sequence):
    tiles = x
    for k in sequence:
        tiles = lax.all_gather(tiles, axes[k])
    done = sequence[::-1]
    back = [done.index(k) for k in range(len(axes))]
    tiles = tiles.transpose(*back, *range(len(axes), tiles.ndim))
    return tiles.reshape(-1, *x.shape)


def whole_of(x, axes, sequence, dim):
    return joined_along(gather_in_order(x, axes, sequence), dim)


def on_device(gradients, master, first_moment, second_moment, old_ratio, group_owner, layer_group):
    layers = old_ratio.shape[0]
    groups = group_owner.shape[0]
    summed = sum_at_owner(gradients.reshape(gradients.shape[2], gradients.shape[3]), REP, 0)
    weight_now = master[0]
    group_ids = lax.broadcasted_iota(jnp.int32, (layers, groups), 1)
    holder = jnp.sum(jnp.where(layer_group[:, None] == group_ids, group_owner[None, :], 0), axis=1)
    my_index = lax.axis_index(SHARD)
    mine = (holder == my_index).astype(jnp.float32)
    my_ratio = jnp.sum(mine * old_ratio)
    new_first = 0.9 * first_moment[0] + 0.1 * summed
    new_second = 0.999 * second_moment[0] + 0.001 * summed * summed
    update = (
        new_first / (1.0 - 0.9**10) / (jnp.sqrt(new_second / (1.0 - 0.999**10)) + 1e-06)
        + 0.1 * weight_now
    )
    new_weight = weight_now - 0.1 * my_ratio * update
    pair = jnp.stack([jnp.sum(weight_now * weight_now), jnp.sum(update * update)])
    table = over_axes(mine[:, None] * pair[None, :], REP_SHARD)
    new_ratio = jnp.sqrt(table[:, 0]) / (jnp.sqrt(table[:, 1]) + 1e-06)
    own_copy = new_weight.astype(jnp.bfloat16)
    every = whole_of(own_copy[None], SHARD, (0, 1, 2), 0)
    replica = jnp.take(every, holder, axis=0)
    return (new_weight[None], new_first[None], new_second[None], replica, new_ratio)


def solution(mesh):
    torus = Mesh(
        mesh.devices.reshape(2, 2, 2, 16, 4), ("rep_0", "rep_1", "shard_0", "shard_1", "shard_2")
    )
    placed = (
        P(REP, SHARD, None, None),
        P(SHARD, REP, None),
        P(SHARD, REP, None),
        P(SHARD, REP, None),
        P(),
        P(),
        P(),
    )
    return jax.shard_map(
        on_device,
        mesh=torus,
        in_specs=placed,
        out_specs=(
            P(SHARD, REP, None),
            P(SHARD, REP, None),
            P(SHARD, REP, None),
            P(None, REP, None),
            P(),
        ),
        check_vma=False,
    )
```

profile of v0, /device:TPU:32, one launch (start us, length us, event | category | flops | bytes accessed | tf_op | source)
XLA Modules:
  0.0 150.1 jit_solution(1895935500783869811)
XLA Ops:
  7.2 0.0 copy-start.2
  7.2 0.0 copy-start.1
  7.2 0.0 copy-start
  7.2 1.7 %reshape_reshape.6 = f32[4,2,5120]{2,1,0:T(2,128)} reshape(f32[1,1,8,5120]{3,2,1,0:T(8,128)} %param.7) | data formatting | bytes 327680 | tf_op jit(solution)/shard_map/reshape;reshape | solution.py:14
  8.9 4.5 %all-to-all-start = ((f32[4,2,5120]{2,1,0:T(2,128)}), f32[4,2,5120]{2,1,0:T(2,128)S(1)}, u32[]{:S(2)}, u32[]{:S(2)}) async-start(f32[4,2,5120]{2,1,0:T(2,128)} %reshape_reshape.6), calls=%async_computation | async-start | bytes 327680 | tf_op jit(solution)/shard_map/all_to_all | solution.py:19
  13.4 0.0 all-gather.4.cloned.1.call-start
  13.4 0.8 select_reduce_fusion
  14.2 1.3 fusion.18
  16.1 3.7 %all-to-all-done = f32[4,2,5120]{2,1,0:T(2,128)S(1)} async-done(((f32[4,2,5120]{2,1,0:T(2,128)}), f32[4,2,5120]{2,1,0:T(2,128)S(1)}, u32[]{:S(2)}, u32[]{:S(2)}) %all-to-all-start) | async-done | bytes 163872 | tf_op jit(solution)/shard_map/all_to_all | solution.py:19
  19.8 0.1 reduce_sum.53
  19.9 1.0 fusion.17
  20.9 4.5 %all_gather.15 = bf16[2,1,2,5120]{3,2,1,0:T(2,128)(2,1)S(1)} all-gather(bf16[1,1,2,5120]{3,2,1,0:T(2,128)(2,1)S(1)} %fusion.17), channel_id=1, replica_groups=mesh['rep_0'=2,'rep_1'=2,'shard_0'=2,'shard_1'=16,'shard_2'=4] {'shard_0'}, dimensions={0}, use_global_device_ids=true | all-gather | bytes 61440 | tf_op jit(solution)/shard_map/all_gather | solution.py:38
  25.3 39.8 %all-gather = bf16[32,1,2,5120]{3,2,1,0:T(2,128)(2,1)} all-gather(bf16[2,1,2,5120]{3,2,1,0:T(2,128)(2,1)S(1)} %all_gather.15), channel_id=2, replica_groups=mesh['rep_0'=2,'rep_1'=2,'shard_0'=2,'shard_1'=16,'shard_2'=4] {'shard_1'}, dimensions={0}, use_global_device_ids=true | all-gather | bytes 696320 | tf_op jit(solution)/shard_map/all_gather | solution.py:38
  65.1 0.0 all-gather.4.cloned.1.call-update
  65.2 1.6 %fusion.8 = f32[]{:T(128)} fusion(f32[2,5120]{1,0:T(2,128)S(1)} %reduce_sum.53, f32[1,2,5120]{2,1,0:T(2,128)} %param.8, f32[1,2,5120]{2,1,0:T(2,128)} %param.10, f32[1,2,5120]{2,1,0:T(2,128)} %param.9), kind=kLoop, calls=%fused_computation.16 | loop fusion | flops 153599 | bytes 163844 | tf_op jit(solution)/shard_map/reduce_sum | solution.py:66
  66.7 0.0 copy-done.2
  66.8 0.0 copy-done.1
  66.8 0.0 copy-done
  66.8 1.4 multiply_subtract_fusion
  68.1 1.4 pad_maximum_fusion
  69.5 0.1 broadcast_multiply_fusion
  69.6 6.4 %psum.35 = f32[128,2]{0,1:T(2,128)S(1)} all-reduce(f32[128,2]{0,1:T(2,128)S(1)} %broadcast_multiply_fusion), channel_id=1, replica_groups=mesh['rep_0'=2,'rep_1'=2,'shard_0'=2,'shard_1'=16,'shard_2'=4] {'rep_0'}, use_global_device_ids=true, to_apply=%region_5.6 | all-reduce | flops 256 | bytes 2048 | tf_op jit(solution)/shard_map/psum | solution.py:25
  76.0 2.4 %psum.36 = f32[128,2]{0,1:T(2,128)S(1)} all-reduce(f32[128,2]{0,1:T(2,128)S(1)} %psum.35), channel_id=1, replica_groups=mesh['rep_0'=2,'rep_1'=2,'shard_0'=2,'shard_1'=16,'shard_2'=4] {'rep_1'}, use_global_device_ids=true, to_apply=%region_6.7 | all-reduce | flops 256 | bytes 2048 | tf_op jit(solution)/shard_map/psum | solution.py:25
  78.4 4.9 %psum.37 = f32[128,2]{0,1:T(2,128)S(1)} all-reduce(f32[128,2]{0,1:T(2,128)S(1)} %psum.36), channel_id=1, replica_groups=mesh['rep_0'=2,'rep_1'=2,'shard_0'=2,'shard_1'=16,'shard_2'=4] {'shard_0'}, use_global_device_ids=true, to_apply=%region_7.8 | all-reduce | flops 256 | bytes 2048 | tf_op jit(solution)/shard_map/psum | solution.py:25
  83.4 28.7 %psum.38 = f32[128,2]{0,1:T(2,128)S(1)} all-reduce(f32[128,2]{0,1:T(2,128)S(1)} %psum.37), channel_id=1, replica_groups=mesh['rep_0'=2,'rep_1'=2,'shard_0'=2,'shard_1'=16,'shard_2'=4] {'shard_1'}, use_global_device_ids=true, to_apply=%region_8.9 | all-reduce | flops 256 | bytes 2048 | tf_op jit(solution)/shard_map/psum | solution.py:25
  112.0 10.5 %psum.39 = f32[128,2]{0,1:T(2,128)S(1)} all-reduce(f32[128,2]{0,1:T(2,128)S(1)} %psum.38), channel_id=1, replica_groups=mesh['rep_0'=2,'rep_1'=2,'shard_0'=2,'shard_1'=16,'shard_2'=4] {'shard_2'}, use_global_device_ids=true, to_apply=%region_9.10 | all-reduce | flops 256 | bytes 2048 | tf_op jit(solution)/shard_map/psum | solution.py:25
  122.5 0.5 fusion.20
  123.0 0.0 all-gather.4.cloned.1.call-done
  123.0 2.5 %copy.19 = bf16[64,2,1,2,5120]{4,0,3,1,2:T(8,128)(2,1)S(1)} copy(bf16[64,2,1,2,5120]{4,3,2,1,0:T(2,128)(2,1)} %all-gather.4.cloned.1.call-done) | data formatting | bytes 5242880 | tf_op jit(solution)/shard_map/all_gather | solution.py:38
  125.6 2.7 %copy.20 = bf16[2,16,4,1,2,5120]{5,4,2,1,0,3:T(2,128)(2,1)S(1)} copy(bf16[2,16,4,1,2,5120]{5,1,2,4,0,3:T(8,128)(2,1)S(1)} %bitcast.79) | data formatting | bytes 5242880 | tf_op jit(solution)/shard_map/transpose | solution.py:41
  128.3 9.3 %gather_fusion = bf16[128,2,5120]{2,1,0:T(2,128)(2,1)} fusion(bf16[128,2,5120]{2,1,0:T(2,128)(2,1)S(1)} %bitcast.78, s32[1024]{0:T(1024)S(1)} %pad_clamp_fusion), kind=kCustom, calls=%fused_computation | custom fusion | bytes 5243392 | tf_op jit(solution)/shard_map/jit(_take)/gather | solution.py:71
  137.5 5.7 %broadcast_select_fusion = bf16[128,2,5120]{2,1,0:T(2,128)(2,1)} fusion(bf16[128,2,5120]{2,1,0:T(2,128)(2,1)} %gather_fusion, pred[128]{0:T(512)(128)(4,1)S(1)} %get-tuple-element.10), kind=kLoop, calls=%fused_computation.1 | loop fusion | flops 1310720 | bytes 5243008 | tf_op jit(solution)/shard_map/jit(_take)/select_n | solution.py:71
  (3 shorter events, 0.0 us)
Async XLA Ops:
  7.2 59.6 %copy-start.2 = (f32[1,2,5120]{2,1,0:T(2,128)S(1)}, f32[1,2,5120]{2,1,0:T(2,128)}, u32[]{:S(2)}) copy-start(f32[1,2,5120]{2,1,0:T(2,128)} %param.10) | copy-start | bytes 122884
  7.2 59.6 %copy-start.1 = (f32[1,2,5120]{2,1,0:T(2,128)S(1)}, f32[1,2,5120]{2,1,0:T(2,128)}, u32[]{:S(2)}) copy-start(f32[1,2,5120]{2,1,0:T(2,128)} %param.9) | copy-start | bytes 122884
  7.2 59.6 %copy-start = (f32[1,2,5120]{2,1,0:T(2,128)S(1)}, f32[1,2,5120]{2,1,0:T(2,128)}, u32[]{:S(2)}) copy-start(f32[1,2,5120]{2,1,0:T(2,128)} %param.8) | copy-start | bytes 122884
  8.9 10.9 %all-to-all-start = ((f32[4,2,5120]{2,1,0:T(2,128)}), f32[4,2,5120]{2,1,0:T(2,128)S(1)}, u32[]{:S(2)}, u32[]{:S(2)}) async-start(f32[4,2,5120]{2,1,0:T(2,128)} %reshape_reshape.6), calls=%async_computation | async-start | bytes 327680 | tf_op jit(solution)/shard_map/all_to_all | solution.py:19
  13.4 109.7 %all-gather.4.cloned.1.call-start = ((), (), s32[]{:S(2)}) async-start(), calls=%async_computation.1 | async-start | bytes 3276800 | tf_op jit(solution)/shard_map/all_gather | solution.py:38
Sparse Core Ops, SparseCore 0:
  65.3 38.0 all-gather.3
where the time goes:
time: 151 us; the launch traced here: 150 us
  blocking collectives  97.2 us (64%)
  local copies, waits for them, and re-layouts  16.2 us (11%)
  between operations  14.8 us (10%)
  other arithmetic  13.8 us (9%)
  starting transfers between devices  4.47 us (3%)
  waiting for transfers between devices  3.7 us (2%)
    psum x5, blocking collectives, over_axes(): x = lax.psum(x, axis)  52.9 us
    all_gather x2, blocking collectives, gather_in_order(): tiles = lax.all_gather(tiles, axes[k])  44.3 us
    gather x1, local copies, waits for them, and re-layouts, on_device(): replica = jnp.take(every, holder, axis=0)  9.25 us
    select_n x2, other arithmetic, on_device(): replica = jnp.take(every, holder, axis=0)  5.69 us
    all_to_all x1, starting transfers between devices, sum_at_owner(): lax.all_to_all(tiles, axis, split_axis=0, concat_axis=0, tiled=True)  4.46 us
    all_to_all x1, waiting for transfers between devices, sum_at_owner(): lax.all_to_all(tiles, axis, split_axis=0, concat_axis=0, tiled=True)  3.68 us
  transfers between devices with their start and end apart: 2, of which 1 were waited for; matrix products, arithmetic and copies ran while one was open for 5% of the time, Pallas kernels for 0%

commit v1 on v0

v1 whole, which is shorter than its diff:
```python
import functools

import jax
import jax.numpy as jnp
from jax import lax
from jax.experimental import pallas as pl
from jax.experimental.pallas import tpu as pltpu
from jax.sharding import Mesh
from jax.sharding import PartitionSpec as P

REP = ("rep_0", "rep_1")
SHARD = ("shard_0", "shard_1", "shard_2")
NX, NY, NZ = 4, 2, 16
SLOTS = NX * NY * NZ
MESH = pl.DeviceIdType.MESH

SCHEDULE = (
    ((0, 0, 0), ((0, 0, -1), (0, 0, 2), (0, 0, 5), (0, 0, -5), (0, 0, 8), (-1, 0, 0), (0, 0, 1), (2, 0, 0), (1, 0, 0), (0, 1, 0),)),
    ((0, 0, -1), ((0, 0, -4), (0, 1, -1), (2, 0, -1), (0, 0, -2), (1, 0, -1), (-1, 0, -1),)),
    ((-1, 0, 0), ((-1, 0, 1), (-1, 1, 0),)),
    ((0, 1, 0), ()),
    ((1, 0, 0), ((1, 1, 0),)),
    ((0, 0, 2), ((0, 1, 2), (2, 0, 2), (0, 0, 3), (-1, 0, 2), (1, 0, 2),)),
    ((2, 0, 0), ((2, 1, 0), (2, 0, 1),)),
    ((0, 0, -5), ((0, 1, -5), (0, 0, -7), (1, 0, -5), (-1, 0, -5), (0, 0, -6),)),
    ((0, 1, -1), ((0, 1, -2), (-1, 1, -1), (1, 1, -1),)),
    ((-1, 0, -1), ()),
    ((1, 0, -1), ((1, 0, -2),)),
    ((-1, 1, 0), ()),
    ((0, 0, 5), ((0, 0, 7), (2, 0, 5), (0, 1, 5), (-1, 0, 5), (0, 0, 6), (1, 0, 5),)),
    ((2, 0, -1), ((2, 1, -1), (2, 0, -2),)),
    ((1, 1, 0), ()),
    ((-1, 0, 2), ((-1, 0, 3),)),
    ((1, 0, 2), ()),
    ((0, 0, 1), ((1, 0, 1), (0, 1, 1),)),
    ((0, 1, 2), ((-1, 1, 2), (1, 1, 2),)),
    ((2, 0, 2), ((2, 0, 3),)),
    ((2, 1, 0), ((2, 1, 1),)),
    ((-1, 0, 1), ((-1, 1, 1),)),
    ((0, 0, -4), ((-1, 0, -4), (1, 0, -4),)),
    ((0, 0, 8), ((0, 1, 8), (-1, 0, 8), (1, 0, 8),)),
    ((0, 0, -2), ((-1, 0, -2), (0, 0, -3),)),
    ((0, 0, 3), ((1, 0, 3), (0, 1, 3), (0, 0, 4),)),
    ((2, 0, 1), ()),
    ((-1, 0, -5), ((-1, 1, -5), (2, 0, -5),)),
    ((1, 0, -5), ((1, 0, -6), (1, 1, -5),)),
    ((0, 1, -5), ((2, 1, -5), (0, 1, -6),)),
    ((-1, 1, -1), ((-1, 1, -2),)),
    ((1, 1, -1), ((1, 1, -2),)),
    ((0, 1, 5), ((-1, 1, 5), (1, 1, 5), (0, 1, 6),)),
    ((0, 0, -7), ((0, 1, -7), (-1, 0, -7), (1, 0, -7),)),
    ((-1, 0, 5), ((-1, 0, 6),)),
    ((1, 0, 5), ()),
    ((2, 1, -1), ((2, 1, -2),)),
    ((0, 0, -6), ((-1, 0, -6),)),
    ((0, 0, 7), ((0, 1, 7), (-1, 0, 7), (1, 0, 7),)),
    ((0, 1, 1), ()),
    ((0, 1, -2), ((0, 1, -3),)),
    ((2, 0, 5), ((2, 0, 6), (2, 1, 5),)),
    ((1, 0, 1), ((1, 1, 1),)),
    ((-1, 1, 2), ((-1, 1, 3), (2, 1, 2),)),
    ((0, 0, 6), ((1, 0, 6),)),
    ((1, 0, -2), ((1, 0, -3),)),
    ((-1, 1, 1), ()),
    ((1, 1, 2), ((1, 1, 3),)),
    ((-1, 0, -4), ((-1, 1, -4), (2, 0, -4),)),
    ((-1, 0, 3), ()),
    ((2, 0, -2), ((2, 0, -3),)),
    ((0, 1, 8), ((1, 1, 8),)),
    ((1, 0, -4), ((1, 1, -4),)),
    ((-1, 0, 8), ((-1, 1, 8),)),
    ((2, 0, 3), ((2, 0, 4), (2, 1, 3),)),
    ((0, 0, -3), ()),
    ((0, 1, 3), ((0, 1, 4),)),
    ((-1, 0, -2), ((-1, 0, -3),)),
    ((1, 0, 8), ((2, 0, 8),)),
    ((2, 1, 1), ()),
    ((1, 0, -6), ((2, 0, -6), (1, 1, -6),)),
    ((-1, 1, -5), ((-1, 1, -6),)),
    ((1, 0, 3), ((1, 0, 4),)),
    ((2, 0, -5), ()),
    ((0, 0, 4), ((-1, 0, 4),)),
    ((0, 1, -6), ()),
    ((1, 1, -5), ()),
    ((0, 1, 6), ()),
    ((-1, 1, 5), ((-1, 1, 6),)),
    ((1, 1, 5), ((1, 1, 6),)),
    ((-1, 1, -2), ((-1, 1, -3),)),
    ((0, 1, -7), ((2, 1, -7),)),
    ((-1, 0, 6), ()),
    ((1, 1, -2), ((1, 1, -3),)),
    ((2, 1, -5), ((2, 1, -6),)),
    ((0, 1, 7), ((-1, 1, 7), (1, 1, 7), (2, 1, 7),)),
    ((-1, 0, -7), ((2, 0, -7), (-1, 1, -7),)),
    ((1, 0, -7), ((1, 1, -7),)),
    ((2, 0, 6), ((2, 1, 6), (2, 0, 7),)),
    ((2, 1, -2), ((2, 1, -3),)),
    ((2, 1, 5), ()),
    ((-1, 0, -6), ()),
    ((1, 0, 7), ()),
    ((-1, 1, 3), ((-1, 1, 4),)),
    ((0, 1, -3), ((0, 1, -4),)),
    ((1, 1, 1), ()),
    ((1, 0, 6), ()),
    ((-1, 0, 7), ()),
    ((1, 1, 3), ((1, 1, 4),)),
    ((1, 0, -3), ()),
    ((-1, 1, -4), ((2, 1, -4),)),
    ((2, 1, 2), ()),
    ((1, 1, 8), ((2, 1, 8),)),
    ((2, 0, 4), ((2, 1, 4),)),
    ((2, 0, -3), ()),
    ((1, 1, -4), ()),
    ((2, 0, -4), ()),
    ((2, 0, 8), ()),
    ((0, 1, 4), ()),
    ((-1, 0, -3), ()),
    ((-1, 1, 8), ()),
    ((-1, 0, 4), ()),
    ((2, 0, -6), ()),
    ((1, 0, 4), ()),
    ((-1, 1, -6), ()),
    ((2, 1, 3), ()),
    ((-1, 1, 6), ()),
    ((-1, 1, -3), ()),
    ((1, 1, -6), ()),
    ((1, 1, 6), ()),
    ((1, 1, -3), ()),
    ((-1, 1, -7), ()),
    ((2, 1, -7), ()),
    ((2, 0, 7), ()),
    ((2, 1, -6), ()),
    ((-1, 1, 7), ()),
    ((1, 1, 7), ()),
    ((1, 1, -7), ()),
    ((-1, 1, 4), ()),
    ((2, 1, -3), ()),
    ((2, 1, 7), ()),
    ((2, 1, 6), ()),
    ((2, 0, -7), ()),
    ((1, 1, 4), ()),
    ((0, 1, -4), ()),
    ((2, 1, 8), ()),
    ((2, 1, 4), ()),
    ((2, 1, -4), ()),
)

PLACES = {row[0]: k for k, row in enumerate(SCHEDULE)}


def step_kernel(
    grad, master, first, second, ratio, owner, group, owner_s, group_s,
    new_master, new_first, new_second, replica, new_ratio,
    gv, parts, mv, fv, sv, rv, ov, lv, os_, ls_, own, buf, stats, table,
    in_sem, rs_send, rs_recv, st_send, st_recv, z_send, z_recv, p_send, p_recv, ag_send, ag_recv,
):
    yh, core, yl, z, x = (lax.axis_index(a) for a in (*REP, *SHARD))
    rep = yh * 2 + core

    def at(dx, dy, dz):
        return (yh, core, lax.rem(yl + dy + 2, NY), lax.rem(z + dz + NZ, NZ), lax.rem(x + dx + NX, NX))

    def slot(dx, dy, dz):
        return lax.rem(yl - dy + 2, NY) * (NZ * NX) + lax.rem(z - dz + NZ, NZ) * NX + lax.rem(x - dx + NX, NX)

    peers = (
        (yh, 1 - core, yl, z, x),
        (1 - yh, core, yl, z, x),
        (1 - yh, 1 - core, yl, z, x),
    )
    line = [(0, 0, dz) for dz in range(1, NZ)]
    plane = [(dx, dy, 0) for dy in range(NY) for dx in range(NX) if dx or dy]

    barrier = pltpu.get_barrier_semaphore()
    partners = [*peers, *(at(*d) for d in line), *(at(*d) for d in plane)]
    for p in partners:
        pl.semaphore_signal(barrier, inc=1, device_id=p, device_id_type=MESH)
    loads = [
        pltpu.make_async_copy(src, dst, in_sem.at[k])
        for k, (src, dst) in enumerate((
            (grad.at[0, 0], gv), (master.at[0], mv), (first.at[0], fv), (second.at[0], sv),
            (ratio, rv), (owner, ov), (group, lv), (owner_s, os_), (group_s, ls_),
        ))
    ]
    for c in loads:
        c.start()
    loads[0].wait()
    for r in range(4):
        parts[r] = gv[2 * r : 2 * r + 2, :]
    pl.semaphore_wait(barrier, len(partners))

    rs = []
    for k, p in enumerate(peers):
        c = pltpu.make_async_remote_copy(
            src_ref=parts.at[p[0] * 2 + p[1]], dst_ref=gv_in(parts, k), send_sem=rs_send.at[k], recv_sem=rs_recv.at[k],
            device_id=p, device_id_type=MESH,
        )
        c.start()
        rs.append(c)
    for c in loads[1:]:
        c.wait()

    me = yl * (NZ * NX) + z * NX + x
    lane = lax.broadcasted_iota(jnp.int32, (1, SLOTS), 1)
    my_group = jnp.sum(jnp.where(ov[...] == me, lane, 0), axis=1, keepdims=True)
    my_ratio = jnp.sum(jnp.where(lv[...] == my_group, rv[...], 0.0), axis=1, keepdims=True)

    for c in rs:
        c.wait_recv()
    ff = mv.shape[1]
    width = ff // 8
    w_acc = jnp.zeros((2, width), jnp.float32)
    u_acc = jnp.zeros((2, width), jnp.float32)
    for b in range(8):
        cols = slice(b * width, (b + 1) * width)
        summed = parts[rep, :, cols] + parts[4, :, cols] + parts[5, :, cols] + parts[6, :, cols]
        w = mv[:, cols]
        nf = 0.9 * fv[:, cols] + 0.1 * summed
        ns = 0.999 * sv[:, cols] + 0.001 * summed * summed
        up = nf / (1.0 - 0.9**10) / (jnp.sqrt(ns / (1.0 - 0.999**10)) + 1e-06) + 0.1 * w
        nw = w - 0.1 * my_ratio * up
        buf[me, :, cols] = nw.astype(jnp.bfloat16)
        new_master[0, :, cols] = nw
        new_first[0, :, cols] = nf
        new_second[0, :, cols] = ns
        w_acc += w * w
        u_acc += up * up

    def send_on(o, children):
        block = buf.at[slot(*o)]
        for c in children:
            d = tuple(b - a for a, b in zip(o, c))
            pltpu.make_async_remote_copy(
                src_ref=block, dst_ref=block, send_sem=ag_send, recv_sem=ag_recv.at[PLACES[c]],
                device_id=at(*d), device_id_type=MESH,
            ).start()

    send_on(*SCHEDULE[0])

    row = lax.broadcasted_iota(jnp.int32, (2, SLOTS), 0)
    w_sum = jnp.sum(w_acc, axis=(0, 1), keepdims=True)
    u_sum = jnp.sum(u_acc, axis=(0, 1), keepdims=True)
    stats[3] = jnp.where(row == 0, w_sum, u_sum)
    st = []
    for k, p in enumerate(peers):
        c = pltpu.make_async_remote_copy(
            src_ref=stats.at[3], dst_ref=stats.at[k], send_sem=st_send.at[k], recv_sem=st_recv.at[k],
            device_id=p, device_id_type=MESH,
        )
        c.start()
        st.append(c)

    here = yl * NX + x

    def stats_to_line():
        for c in st:
            c.wait_recv()
        table[here, z] = stats[0] + stats[1] + stats[2] + stats[3]
        for d in line:
            pltpu.make_async_remote_copy(
                src_ref=table.at[here, z], dst_ref=table.at[here, z], send_sem=z_send, recv_sem=z_recv,
                device_id=at(*d), device_id_type=MESH,
            ).start()

    def stats_to_plane():
        some = table.at[0, 0 : NZ - 1]
        pltpu.make_async_copy(some, some, z_recv).wait()
        for d in plane:
            pltpu.make_async_remote_copy(
                src_ref=table.at[here], dst_ref=table.at[here], send_sem=p_send, recv_sem=p_recv,
                device_id=at(*d), device_id_type=MESH,
            ).start()

    def wait_for(o):
        block = buf.at[slot(*o)]
        pltpu.make_async_copy(block, block, ag_recv.at[PLACES[o]]).wait()

    for k, (o, children) in enumerate(SCHEDULE[1:]):
        if k == LINE_AT:
            stats_to_line()
        if k == PLANE_AT:
            stats_to_plane()
        wait_for(o)
        send_on(o, children)

    some = table.at[0 : NX * NY - 1]
    pltpu.make_async_copy(some, some, p_recv).wait()

    sub = lax.broadcasted_iota(jnp.int32, (SLOTS, SLOTS), 0)
    lan = lax.broadcasted_iota(jnp.int32, (SLOTS, SLOTS), 1)
    owner_col = jnp.sum(jnp.where(sub == lan, ov[...], 0), axis=1, keepdims=True)
    holder = jnp.sum(jnp.where(sub == lv[...], owner_col, 0), axis=0, keepdims=True)
    place = ((holder // (NZ * NX)) * NX + lax.rem(holder, NX)) * NZ + lax.rem(holder // NX, NZ)
    picked = jnp.zeros((2, SLOTS), jnp.float32)
    for p in range(SLOTS):
        picked = jnp.where(place == p, table[p // NZ, p % NZ], picked)
    new_ratio[...] = jnp.sqrt(picked[0:1]) / (jnp.sqrt(picked[1:2]) + 1e-06)

    def put(l, carry):
        replica[l] = buf[os_[ls_[l]]]
        return carry

    lax.fori_loop(0, SLOTS, put, 0, unroll=8)

    for c in rs:
        c.wait_send()
    for c in st:
        c.wait_send()
    some = table.at[0, 0 : NZ - 1]
    pltpu.make_async_copy(some, some, z_send).wait()
    some = table.at[0 : NX * NY - 1]
    pltpu.make_async_copy(some, some, p_send).wait()
    some = buf.at[0 : SLOTS - 1]
    pltpu.make_async_copy(some, some, ag_send).wait()


def gv_in(parts, k):
    return parts.at[4 + k]


LINE_AT = 8
PLANE_AT = 60


def flush_kernel(a, b, c, d, e, a_out, b_out, c_out, d_out, e_out, sem):
    copies = [
        pltpu.make_async_copy(src, dst, sem.at[k])
        for k, (src, dst) in enumerate(((d, d_out), (a, a_out), (b, b_out), (c, c_out), (e, e_out)))
    ]
    for copy in copies:
        copy.start()
    for copy in copies:
        copy.wait()


def on_device(gradients, master, first_moment, second_moment, old_ratio, group_owner, layer_group):
    ff = master.shape[2]
    f32, i32 = jnp.float32, jnp.int32
    hbm, vmem = pl.BlockSpec(memory_space=pltpu.HBM), pl.BlockSpec(memory_space=pltpu.VMEM)
    shapes = (
        jax.ShapeDtypeStruct(master.shape, f32),
        jax.ShapeDtypeStruct(master.shape, f32),
        jax.ShapeDtypeStruct(master.shape, f32),
        jax.ShapeDtypeStruct((SLOTS, 2, ff), jnp.bfloat16),
        jax.ShapeDtypeStruct((1, SLOTS), f32),
    )
    dma = pltpu.SemaphoreType.DMA
    results = pl.pallas_call(
        step_kernel,
        out_shape=shapes,
        in_specs=[hbm] * 9,
        out_specs=[vmem] * 5,
        scratch_shapes=[
            pltpu.VMEM((8, ff), f32),
            pltpu.VMEM((7, 2, ff), f32),
            pltpu.VMEM((2, ff), f32),
            pltpu.VMEM((2, ff), f32),
            pltpu.VMEM((2, ff), f32),
            pltpu.VMEM((1, SLOTS), f32),
            pltpu.VMEM((1, SLOTS), i32),
            pltpu.VMEM((1, SLOTS), i32),
            pltpu.SMEM((SLOTS,), i32),
            pltpu.SMEM((SLOTS,), i32),
            pltpu.VMEM((2, ff), jnp.bfloat16),
            pltpu.VMEM((SLOTS, 2, ff), jnp.bfloat16),
            pltpu.VMEM((4, 2, SLOTS), f32),
            pltpu.VMEM((NX * NY, NZ, 2, SLOTS), f32),
            dma((9,)),
            dma((3,)),
            dma((3,)),
            dma((3,)),
            dma((3,)),
            dma,
            dma,
            dma,
            dma,
            dma,
            dma((SLOTS,)),
        ],
        compiler_params=pltpu.CompilerParams(
            collective_id=0, has_side_effects=True, vmem_limit_bytes=24 << 20
        ),
        name="lamb_step",
    )(
        gradients, master, first_moment, second_moment,
        old_ratio.reshape(1, SLOTS), group_owner.reshape(1, SLOTS), layer_group.reshape(1, SLOTS),
        group_owner, layer_group,
    )
    a, b, c, d, e = pl.pallas_call(
        flush_kernel,
        out_shape=shapes,
        in_specs=[vmem] * 5,
        out_specs=[hbm] * 5,
        scratch_shapes=[dma((5,))],
        compiler_params=pltpu.CompilerParams(vmem_limit_bytes=16 << 20),
        name="lamb_flush",
    )(*results)
    return a, b, c, d, e.reshape(SLOTS)


def solution(mesh):
    torus = Mesh(mesh.devices.reshape(2, 2, NY, NZ, NX), (*REP, *SHARD))
    placed = (
        P(REP, SHARD, None, None),
        P(SHARD, REP, None),
        P(SHARD, REP, None),
        P(SHARD, REP, None),
        P(),
        P(),
        P(),
    )
    return jax.shard_map(
        on_device,
        mesh=torus,
        in_specs=placed,
        out_specs=(P(SHARD, REP, None), P(SHARD, REP, None), P(SHARD, REP, None), P(None, REP, None), P()),
        check_vma=False,
    )
```

time: 151 us -> 50.3 us (0.33)
  the two profiles are of different devices: /device:TPU:32 before, /device:TPU:8 now
where the time goes in v1:
time: 50.3 us; the launch traced here: 49.9 us
  Pallas kernels  44.1 us (88%)
  local copies, waits for them, and re-layouts  5.21 us (10%)
  between operations  0.66 us (1%)
    pallas_call x1, Pallas kernels, on_device(): pl.pallas_call(step_kernel, out_shape=shapes, in_specs=[hbm] * 9, out_spe...  42.5 us
    unnamed x14, local copies, waits for them, and re-layouts  5.21 us
    pallas_call x1, Pallas kernels, on_device(): pl.pallas_call(flush_kernel, out_shape=shapes, in_specs=[vmem] * 5, out_s...  1.56 us

profile of v1, /device:TPU:8, one launch (start us, length us, event | category | flops | bytes accessed | tf_op | source)
XLA Modules:
  0.0 49.9 jit_solution(17247772008373760127)
XLA Ops:
  0.6 0.0 copy-start
  0.6 0.9 %copy-done = f32[1,1,8,5120]{3,2,1,0:T(8,128)S(1)} copy-done((f32[1,1,8,5120]{3,2,1,0:T(8,128)S(1)}, f32[1,1,8,5120]{3,2,1,0:T(8,128)}, u32[]{:S(2)}) %copy-start) | copy-done | bytes 163864
  1.6 0.0 copy-start.1
  1.6 0.8 %copy-done.1 = f32[1,2,5120]{2,1,0:T(2,128)S(1)} copy-done((f32[1,2,5120]{2,1,0:T(2,128)S(1)}, f32[1,2,5120]{2,1,0:T(2,128)}, u32[]{:S(2)}) %copy-start.1) | copy-done | bytes 40984
  2.3 0.0 copy-start.2
  2.3 0.8 %copy-done.2 = f32[1,2,5120]{2,1,0:T(2,128)S(1)} copy-done((f32[1,2,5120]{2,1,0:T(2,128)S(1)}, f32[1,2,5120]{2,1,0:T(2,128)}, u32[]{:S(2)}) %copy-start.2) | copy-done | bytes 40984
  3.1 0.0 copy-start.3
  3.1 0.8 %copy-done.3 = f32[1,2,5120]{2,1,0:T(2,128)S(1)} copy-done((f32[1,2,5120]{2,1,0:T(2,128)S(1)}, f32[1,2,5120]{2,1,0:T(2,128)}, u32[]{:S(2)}) %copy-start.3) | copy-done | bytes 40984
  3.9 0.0 copy-start.4
  3.9 0.7 %copy-done.4 = s32[128]{0:T(128)S(1)} copy-done((s32[128]{0:T(128)S(1)}, s32[128]{0:T(128)}, u32[]{:S(2)}) %copy-start.4) | copy-done | bytes 536
  4.5 0.0 copy-start.5
  4.5 0.7 %copy-done.5 = s32[128]{0:T(128)S(1)} copy-done((s32[128]{0:T(128)S(1)}, s32[128]{0:T(128)}, u32[]{:S(2)}) %copy-start.5) | copy-done | bytes 536
  5.2 0.0 copy-start.6
  5.2 0.7 %copy-done.6 = f32[128]{0:T(128)S(1)} copy-done((f32[128]{0:T(128)S(1)}, f32[128]{0:T(128)}, u32[]{:S(2)}) %copy-start.6) | copy-done | bytes 536
  5.9 42.5 %lamb_step.1 = (f32[1,2,5120]{2,1,0:T(2,128)S(1)}, f32[1,2,5120]{2,1,0:T(2,128)S(1)}, f32[1,2,5120]{2,1,0:T(2,128)S(1)}, bf16[128,2,5120]{2,1,0:T(2,128)(2,1)S(1)}, f32[1,128]{1,0:T(1,128)S(1)}) custom-call(f32[1,1,8,5120]{3,2,1,0:T(8,128)S(1)} %copy-done, f32[1,2,5120]{2,1,0:T(2,128)S(1)} %copy-done.1, f32[1,2,5120]{2,1,0:T(2,128)S(1)} %copy-done.2, ...), custom_call_target="tpu_custom_call" | custom-call | tf_op jit(solution)/shard_map/lamb_step/pallas_call | solution.py:348
  48.4 1.6 %lamb_flush.1 = (f32[1,2,5120]{2,1,0:T(2,128)}, f32[1,2,5120]{2,1,0:T(2,128)}, f32[1,2,5120]{2,1,0:T(2,128)}, bf16[128,2,5120]{2,1,0:T(2,128)(2,1)}, f32[1,128]{1,0:T(1,128)}) custom-call(f32[1,2,5120]{2,1,0:T(2,128)S(1)} %get-tuple-element.15.a, f32[1,2,5120]{2,1,0:T(2,128)S(1)} %get-tuple-element.16.b, f32[1,2,5120]{2,1,0:T(2,128)S(1)} %get-tuple-element.17.c, ...), custom_call_target="tpu_custom_call" | custom-call | tf_op jit(solution)/shard_map/lamb_flush/pallas_call | solution.py:389
Async XLA Ops:
  0.6 0.9 %copy-start = (f32[1,1,8,5120]{3,2,1,0:T(8,128)S(1)}, f32[1,1,8,5120]{3,2,1,0:T(8,128)}, u32[]{:S(2)}) copy-start(f32[1,1,8,5120]{3,2,1,0:T(8,128)} %grad.1) | copy-start | bytes 491524
  1.6 0.8 %copy-start.1 = (f32[1,2,5120]{2,1,0:T(2,128)S(1)}, f32[1,2,5120]{2,1,0:T(2,128)}, u32[]{:S(2)}) copy-start(f32[1,2,5120]{2,1,0:T(2,128)} %master.1) | copy-start | bytes 122884
  2.3 0.8 %copy-start.2 = (f32[1,2,5120]{2,1,0:T(2,128)S(1)}, f32[1,2,5120]{2,1,0:T(2,128)}, u32[]{:S(2)}) copy-start(f32[1,2,5120]{2,1,0:T(2,128)} %first.1) | copy-start | bytes 122884
  3.1 0.8 %copy-start.3 = (f32[1,2,5120]{2,1,0:T(2,128)S(1)}, f32[1,2,5120]{2,1,0:T(2,128)}, u32[]{:S(2)}) copy-start(f32[1,2,5120]{2,1,0:T(2,128)} %second.1) | copy-start | bytes 122884
  3.9 0.7 %copy-start.4 = (s32[128]{0:T(128)S(1)}, s32[128]{0:T(128)}, u32[]{:S(2)}) copy-start(s32[128]{0:T(128)} %owner_s.1) | copy-start | bytes 1540
  4.5 0.7 %copy-start.5 = (s32[128]{0:T(128)S(1)}, s32[128]{0:T(128)}, u32[]{:S(2)}) copy-start(s32[128]{0:T(128)} %group_s.1) | copy-start | bytes 1540
  5.2 0.7 %copy-start.6 = (f32[128]{0:T(128)S(1)}, f32[128]{0:T(128)}, u32[]{:S(2)}) copy-start(f32[128]{0:T(128)} %param.11) | copy-start | bytes 1540
